TPU v7x, 512 devices: a 8x2x16 block of a 8x8x16 slice. The times are simulated.
512 devices in a mesh: subj: 2 (over y), row: 16 (over x, core), col: 16 (over z).
Axes of the slice: x: 8, y: 2, z: 16, core: 2. Of those that a mesh axis runs over, the one named last changes fastest.
The devices are a block of a 8x8x16 slice.
Arguments:
- series: float32 [800, 65536], P(None, ('subj', 'row', 'col')), parts along dimension 1, as said below
- keep_mask: int32 [512, 256], P(('subj', 'row'), 'col'), parts along dimension 0, may hold values from 0 to 1, as said below
- row_owner: int32 [512], P('subj'), parts along dimension 0, may hold values from 0 to 15, as said below
Outputs:
- owned_tiles: bfloat16 [32, 16, 96, 128, 128], P(('subj', 'row'), 'col'), parts along dimension 0
- owned_ids: int32 [32, 16, 96], P(('subj', 'row'), 'col'), parts along dimension 0
There are 2 independent parts, one for each index of `subj`. A program takes and returns all parts, laid end to end along the dimension named above; each array names one. Nothing has to cross between parts.
Inputs may be any that keep to these rules, and one draw needn't show every extreme that they name: Each voxel's series varies over time. `keep_mask`: of the 16 tiles that one tile row has in one column block, at most 6 are kept; in every draw one owner keeps exactly 6 in each of its tile rows in some column block. `row_owner`: the 16 tile rows of a row block have 16 different owners, and every owner holds 16 tile rows, from 16 different row blocks.
All inputs are finite; a program needn't handle non-finite values.
Results may differ from a plain program's by a relative error of at most 0.0042.
Values may be sent and summed in bfloat16 or wider, within the bound.
No kernel may reach another device: no remote copies, remote signals or barrier semaphores. Data moves between devices by JAX's collectives and lax.ppermute only.
A program may use at most 64 MiB of HBM per device.

v0:
```python
import jax
import jax.numpy as jnp
from jax import lax
from jax.sharding import PartitionSpec as P

TILE = 128
epsilon = 1e-05


def compact(flat_tiles, flat_ids, capacity):
    is_valid = (flat_ids >= 0).astype(jnp.int32)
    running = jnp.cumsum(is_valid)
    slot_index = jnp.arange(capacity, dtype=jnp.int32)
    position = jnp.arange(flat_ids.shape[0], dtype=jnp.int32)
    slot_hit = (is_valid[None, :] == 1) & (running[None, :] == slot_index[:, None] + 1)
    picked = jnp.sum(jnp.where(slot_hit, position[None, :], 0), axis=1)
    present = running[-1] > slot_index
    chosen = jnp.take(flat_tiles, picked, axis=0)
    slot_tiles = jnp.where(present[:, None, None], chosen, jnp.zeros_like(chosen))
    slot_ids = jnp.where(present, jnp.take(flat_ids, picked), -1).astype(jnp.int32)
    return (slot_tiles, slot_ids)


def shards(series, keep_mask, row_owner):
    frames = series.shape[0]
    average = jnp.mean(series, axis=0, keepdims=True)
    centred = series - average
    spread = jnp.mean(centred * centred, axis=0, keepdims=True)
    scored = (centred * lax.rsqrt(spread + epsilon)).astype(jnp.bfloat16)
    row_block = lax.all_gather(scored, "col", axis=1, tiled=True)
    product = lax.dot_general(
        row_block,
        lax.all_gather(scored, "row", axis=1, tiled=True),
        (((0,), (0,)), ((), ())),
        preferred_element_type=jnp.float32,
    )
    tile_grid = (product * (1.0 / frames)).astype(jnp.bfloat16)
    row_count, col_count = keep_mask.shape
    tile_grid = tile_grid.reshape(row_count, TILE, col_count, TILE).transpose(0, 2, 1, 3)
    row_devices = lax.axis_size("row")
    col_devices = lax.axis_size("col")
    row_index = lax.axis_index("row")
    col_index = lax.axis_index("col")
    total_cols = col_count * col_devices
    slot_limit = max(2, 3 * col_count // 8)
    capacity = row_count * slot_limit
    local_owner = lax.dynamic_slice_in_dim(row_owner, row_index * row_count, row_count)
    targets = jnp.arange(row_devices, dtype=jnp.int32)
    owns_row = local_owner[None, :] == targets[:, None]
    has_row = jnp.any(owns_row, axis=1)
    row_of = jnp.sum(
        jnp.where(owns_row, jnp.arange(row_count, dtype=jnp.int32)[None, :], 0), axis=1
    )
    keep_flags = jnp.where(has_row[:, None], jnp.take(keep_mask, row_of, axis=0), 0)
    global_row = row_index * row_count + row_of
    first_col = col_index * col_count
    running = jnp.cumsum(keep_flags, axis=1)
    slot_index = jnp.arange(slot_limit, dtype=jnp.int32)
    slot_hit = (keep_flags[:, None, :] == 1) & (
        running[:, None, :] == slot_index[None, :, None] + 1
    )
    picked = jnp.sum(
        jnp.where(slot_hit, jnp.arange(col_count, dtype=jnp.int32)[None, None, :], 0), axis=2
    )
    present = running[:, -1:] > slot_index[None, :]
    chosen = tile_grid[row_of[:, None], picked]
    outgoing = jnp.where(present[:, :, None, None], chosen, jnp.zeros_like(chosen))
    out_ids = jnp.where(present, global_row[:, None] * total_cols + first_col + picked, -1)
    incoming, in_ids = (
        lax.all_to_all(outgoing, "row", split_axis=0, concat_axis=0, tiled=True),
        lax.all_to_all(out_ids, "row", split_axis=0, concat_axis=0, tiled=True),
    )
    flat_tiles = incoming.reshape(-1, TILE, TILE)
    flat_ids = in_ids.reshape(-1)
    slot_tiles, slot_ids = compact(flat_tiles, flat_ids, capacity)
    return (slot_tiles.reshape(1, 1, capacity, TILE, TILE), slot_ids.reshape(1, 1, capacity))


def solution(mesh):
    in_specs = (P(None, ("subj", "row", "col")), P(("subj", "row"), "col"), P("subj"))
    out_specs = (P(("subj", "row"), "col", None, None, None), P(("subj", "row"), "col", None))
    return jax.shard_map(shards, mesh=mesh, in_specs=in_specs, out_specs=out_specs, check_vma=False)
```

profile of v0, /device:TPU:65, one launch (start us, length us, event | category | flops | bytes accessed | tf_op | source)
XLA Modules:
  0.0 313.3 jit_solution(12894685114126903149)
XLA Ops:
  7.3 1.1 reduce_sum.60
  8.4 1.1 multiply_reduce_fusion
  9.5 1.7 multiply_convert_fusion.1
  11.4 0.7 all-gather.5.cloned.1.call-update
  12.1 0.8 dynamic_slice.3
  12.9 0.1 select_reduce_fusion.2
  13.0 0.6 gather_fusion
  13.6 0.1 fusion.3
  13.8 0.2 reduce_window_sum.18
  14.0 0.2 slice_reduce_fusion
  14.2 0.3 select_reduce_fusion.1
  14.4 0.7 copy.18
  15.1 44.6 %all-to-all-start = ((s32[16,1,6]{2,1,0:T(1,128)}), s32[16,1,6]{2,1,0:T(1,128)S(1)}, u32[]{:S(2)}, u32[]{:S(2)}) async-start(s32[16,1,6]{2,1,0:T(1,128)} %copy.18), calls=%async_computation | async-start | bytes 16384 | tf_op jit(solution)/shard_map/all_to_all | solution.py:71
  60.0 64.0 %all-gather.3.cloned.1.call-done = bf16[800,2048]{1,0:T(8,128)(2,1)} async-done(((bf16[800,128]{1,0:T(8,128)(2,1)}), bf16[800,2048]{1,0:T(8,128)(2,1)}) %all-gather.3.cloned.1.call-update) | async-done | bytes 3276816 | tf_op jit(solution)/shard_map/all_gather | solution.py:30
  124.0 61.5 %all-gather.5.cloned.1.call-done = bf16[800,2048]{1,0:T(8,128)(2,1)} async-done(((bf16[800,128]{1,0:T(8,128)(2,1)}), bf16[800,2048]{1,0:T(8,128)(2,1)}) %all-gather.5.cloned.1.call-update) | async-done | bytes 3276816 | tf_op jit(solution)/shard_map/all_gather | solution.py:33
  185.5 13.6 %fusion = bf16[256,8,16,128]{3,1,2,0:T(8,128)(2,1)} fusion(bf16[800,2048]{1,0:T(8,128)(2,1)} %all-gather.3.cloned.1.call-done, bf16[800,2048]{1,0:T(8,128)(2,1)} %all-gather.5.cloned.1.call-done), kind=kOutput, calls=%fused_computation.6 | convolution fusion | flops 6719275008 | bytes 14942208 | tf_op jit(solution)/shard_map/dot_general | solution.py:31
  199.2 9.7 %copy.22 = bf16[256,8,16,128]{3,2,1,0:T(8,128)(2,1)} copy(bf16[256,8,16,128]{3,1,2,0:T(8,128)(2,1)} %fusion) | data formatting | bytes 16777216
  208.9 9.1 %copy.24 = bf16[16,128,16,128]{3,1,2,0:T(8,128)(2,1)} copy(bf16[16,128,16,128]{3,2,1,0:T(8,128)(2,1)} %bitcast.36) | data formatting | bytes 16777216 | tf_op jit(solution)/shard_map/reshape | solution.py:39
  218.0 4.9 %gather_fusion.1 = bf16[96,128,128]{2,1,0:T(8,128)(2,1)S(1)} fusion(bf16[16,16,128,128]{3,2,1,0:T(8,128)(2,1)} %bitcast.37, s32[96]{0:T(128)S(1)} %reshape.311), kind=kCustom, calls=%fused_computation.1 | custom fusion | bytes 6292224 | tf_op jit(solution)/shard_map/gather | solution.py:66
  223.0 1.9 broadcast_select_fusion
  224.9 4.5 %all-to-all-start.1 = ((bf16[16,6,128,128]{3,2,1,0:T(8,128)(2,1)}), bf16[16,6,128,128]{3,2,1,0:T(8,128)(2,1)S(1)}, u32[]{:S(2)}, u32[]{:S(2)}) async-start(bf16[16,6,128,128]{3,2,1,0:T(8,128)(2,1)} %broadcast_select_fusion), calls=%async_computation.1 | async-start | bytes 6291456 | tf_op jit(solution)/shard_map/all_to_all | solution.py:70
  229.4 0.5 broadcast.364
  229.9 0.7 fusion.11
  230.7 0.1 reduce-window.4
  230.9 0.6 slice.21
  231.6 0.2 select_reduce_fusion
  231.8 1.2 gather_fusion.3
  233.1 0.7 compare_and_fusion
  233.8 1.2 compare_select_fusion.6
  235.0 65.3 %all-to-all-done.1 = bf16[16,6,128,128]{3,2,1,0:T(8,128)(2,1)S(1)} async-done(((bf16[16,6,128,128]{3,2,1,0:T(8,128)(2,1)}), bf16[16,6,128,128]{3,2,1,0:T(8,128)(2,1)S(1)}, u32[]{:S(2)}, u32[]{:S(2)}) %all-to-all-start.1) | async-done | bytes 3145760 | tf_op jit(solution)/shard_map/all_to_all | solution.py:70
  300.3 2.7 gather_fusion.2
  303.0 3.4 %fusion.1 = bf16[1,1,96,128,128]{4,3,2,1,0:T(8,128)(2,1)} fusion(bf16[96,128,128]{2,1,0:T(8,128)(2,1)} %gather_fusion.2, pred[96]{0:T(512)(128)(4,1)S(1)} %get-tuple-element.8, pred[96]{0:T(512)(128)(4,1)S(1)} %get-tuple-element.9), kind=kLoop, calls=%fused_computation.8 | loop fusion | flops 3145728 | bytes 6291648 | tf_op jit(solution)/shard_map/jit(_where)/select_n | solution.py:19
  (26 shorter events, 0.9 us)
Async XLA Ops:
  7.2 5.9 %copy-start = (s32[16,16]{1,0:T(8,128)S(1)}, s32[16,16]{1,0:T(8,128)}, u32[]{:S(2)}) copy-start(s32[16,16]{1,0:T(8,128)} %param.4) | copy-start | bytes 3076
  7.2 116.8 %all-gather.3.cloned.1.call-start = ((), (), s32[]{:S(2)}) async-start(), calls=%async_computation.2 | async-start | bytes 3481600 | tf_op jit(solution)/shard_map/all_gather | solution.py:30
  11.3 174.2 %all-gather.5.cloned.1.call-start = ((), (), s32[]{:S(2)}) async-start(), calls=%async_computation.3 | async-start | bytes 3481600 | tf_op jit(solution)/shard_map/all_gather | solution.py:33
  15.1 209.8 %all-to-all-start = ((s32[16,1,6]{2,1,0:T(1,128)}), s32[16,1,6]{2,1,0:T(1,128)S(1)}, u32[]{:S(2)}, u32[]{:S(2)}) async-start(s32[16,1,6]{2,1,0:T(1,128)} %copy.18), calls=%async_computation | async-start | bytes 16384 | tf_op jit(solution)/shard_map/all_to_all | solution.py:71
  224.9 75.4 %all-to-all-start.1 = ((bf16[16,6,128,128]{3,2,1,0:T(8,128)(2,1)}), bf16[16,6,128,128]{3,2,1,0:T(8,128)(2,1)S(1)}, u32[]{:S(2)}, u32[]{:S(2)}) async-start(bf16[16,6,128,128]{3,2,1,0:T(8,128)(2,1)} %broadcast_select_fusion), calls=%async_computation.1 | async-start | bytes 6291456 | tf_op jit(solution)/shard_map/all_to_all | solution.py:70
Sparse Core Ops, SparseCore 0:
  11.4 112.5 all-gather.2
  126.6 58.8 all-gather.4
where the time goes:
time: 314 us; the launch traced here: 313 us
  waiting for transfers between devices  192 us (61%)
  starting transfers between devices  49.2 us (16%)
  local copies, waits for them, and re-layouts  31.4 us (10%)
  between operations  14.2 us (5%)
  matrix products  13.6 us (4%)
  other arithmetic  13.2 us (4%)
    all_to_all x1, waiting for transfers between devices, shards(): lax.all_to_all(outgoing, 'row', split_axis=0, concat_axis=0, tiled=True)  65.3 us
    all_gather x1, waiting for transfers between devices, shards(): row_block = lax.all_gather(scored, 'col', axis=1, tiled=True)  64 us
    all_gather x1, waiting for transfers between devices, shards(): lax.all_gather(scored, 'row', axis=1, tiled=True)  61.5 us
    all_to_all x1, starting transfers between devices, shards(): lax.all_to_all(out_ids, 'row', split_axis=0, concat_axis=0, tiled=True)  44.6 us
    dot_general x1, matrix products, shards(): lax.dot_general(row_block, lax.all_gather(scored, 'row', axis=1, tiled=Tr...  13.6 us
    unnamed x3, local copies, waits for them, and re-layouts  9.76 us
    reshape x1, local copies, waits for them, and re-layouts, shards(): tile_grid.reshape(row_count, TILE, col_count, TILE).transpose(0, 2, 1, 3)  9.11 us
  transfers between devices with their start and end apart: 4, of which 3 were waited for; matrix products, arithmetic and copies ran while one was open for 15% of the time, Pallas kernels for 0%

commit v1 on v0

--- a/solution.py
+++ b/solution.py
@@ -27,7 +27,16 @@
     centred = series - average
     spread = jnp.mean(centred * centred, axis=0, keepdims=True)
     scored = (centred * lax.rsqrt(spread + epsilon)).astype(jnp.bfloat16)
-    row_block = lax.all_gather(scored, "col", axis=1, tiled=True)
+    ways = lax.axis_size("col")
+    up = [(d, (d + 1) % ways) for d in range(ways)]
+    down = [(d, (d - 1) % ways) for d in range(ways)]
+    earlier, later = ([scored], [scored])
+    for _ in range(ways // 2):
+        earlier.append(lax.ppermute(earlier[-1], "col", up))
+    for _ in range((ways - 1) // 2):
+        later.append(lax.ppermute(later[-1], "col", down))
+    line = jnp.concatenate([*earlier[::-1], *later[1:]], axis=1)
+    row_block = jnp.roll(line, (lax.axis_index("col") - ways // 2) * scored.shape[1], axis=1)
     product = lax.dot_general(
         row_block,
         lax.all_gather(scored, "row", axis=1, tiled=True),

time: 314 us -> 288 us (0.917)
  waiting for transfers between devices: 192 us -> 77.4 us
  starting transfers between devices: 49.2 us -> 113 us
  local copies, waits for them, and re-layouts: 31.4 us -> 53.1 us
    ppermute x0 -> x15, starting transfers between devices: none -> 90.2 us  [the longest x7 70.1 us: shards(): later.append(lax.ppermute(later[-1], 'col', down))]
    all_gather x1 -> x0, waiting for transfers between devices: 64 us -> none  [shards(): row_block = lax.all_gather(scored, 'col', axis=1, tiled=True)]
    all_gather x1, waiting for transfers between devices: 61.5 us -> 0.01 us  [shards(): lax.all_gather(scored, 'row', axis=1, tiled=True)]
    all_to_all x1, starting transfers between devices: 44.6 us -> 14 us  [shards(): lax.all_to_all(out_ids, 'row', split_axis=0, concat_axis=0, tiled=True)]
    unnamed x3 -> x36, local copies, waits for them, and re-layouts: 9.76 us -> 30.8 us
    ppermute x0 -> x15, waiting for transfers between devices: none -> 12 us  [the longest x8 8.86 us: shards(): earlier.append(lax.ppermute(earlier[-1], 'col', up))]
    all_to_all x1, starting transfers between devices: 4.46 us -> 9.11 us  [shards(): lax.all_to_all(outgoing, 'row', split_axis=0, concat_axis=0, tiled=True)]
  transfers between devices with their start and end apart: 4 -> 18, of which waited for: 3 -> 8; matrix products, arithmetic and copies ran while one was open for 15% -> 25% of each run, Pallas kernels for 0% -> 0%
where the time goes in v1:
time: 288 us; the launch traced here: 287 us
  starting transfers between devices  113 us (39%)
  waiting for transfers between devices  77.4 us (27%)
  local copies, waits for them, and re-layouts  53.1 us (18%)
  other arithmetic  15.2 us (5%)
  between operations  14.4 us (5%)
  matrix products  13.6 us (5%)
    ppermute x7, starting transfers between devices, shards(): later.append(lax.ppermute(later[-1], 'col', down))  70.1 us
    all_to_all x1, waiting for transfers between devices, shards(): lax.all_to_all(outgoing, 'row', split_axis=0, concat_axis=0, tiled=True)  65.3 us
    unnamed x36, local copies, waits for them, and re-layouts  30.8 us
    ppermute x8, starting transfers between devices, shards(): earlier.append(lax.ppermute(earlier[-1], 'col', up))  20.2 us
    all_to_all x1, starting transfers between devices, shards(): lax.all_to_all(out_ids, 'row', split_axis=0, concat_axis=0, tiled=True)  14 us
    dot_general x1, matrix products, shards(): lax.dot_general(row_block, lax.all_gather(scored, 'row', axis=1, tiled=Tr...  13.6 us
    all_to_all x1, starting transfers between devices, shards(): lax.all_to_all(outgoing, 'row', split_axis=0, concat_axis=0, tiled=True)  9.11 us
    reshape x1, local copies, waits for them, and re-layouts, shards(): tile_grid.reshape(row_count, TILE, col_count, TILE).transpose(0, 2, 1, 3)  9.11 us
  transfers between devices with their start and end apart: 18, of which 8 were waited for; matrix products, arithmetic and copies ran while one was open for 25% of the time, Pallas kernels for 0%

profile of v1, /device:TPU:65, one launch (start us, length us, event | category | flops | bytes accessed | tf_op | source)
XLA Modules:
  0.0 287.0 jit_solution(9035037917380059363)
XLA Ops:
  7.3 1.2 reduce_sum.60
  10.6 6.6 %collective-permute-start = (bf16[800,128]{1,0:T(8,128)(2,1)S(1)}, bf16[800,128]{1,0:T(8,128)(2,1)S(1)}, u32[]{:S(2)}, u32[]{:S(2)}) collective-permute-start(bf16[800,128]{1,0:T(8,128)(2,1)S(1)} %multiply_convert_fusion.1), channel_id=1, source_target_pairs={{0,1},{1,2},{2,3},{3,4},{4,5},{5,6},{6,7},{7,8},{8,9},{9,10},{10,1... | collective-permute-start | bytes 614408 | tf_op jit(solution)/shard_map/ppermute | solution.py:35
  17.2 39.9 %collective-permute-start.8 = (bf16[800,128]{1,0:T(8,128)(2,1)S(1)}, bf16[800,128]{1,0:T(8,128)(2,1)S(1)}, u32[]{:S(2)}, u32[]{:S(2)}) collective-permute-start(bf16[800,128]{1,0:T(8,128)(2,1)S(1)} %multiply_convert_fusion.1), channel_id=1, source_target_pairs={{0,15},{1,0},{2,1},{3,2},{4,3},{5,4},{6,5},{7,6},{8,7},{9,8},{10,9... | collective-permute-start | bytes 614408 | tf_op jit(solution)/shard_map/ppermute | solution.py:37
  58.9 1.9 collective-permute-start.1
  60.9 5.8 %collective-permute-done.1 = bf16[800,128]{1,0:T(8,128)(2,1)S(1)} collective-permute-done((bf16[800,128]{1,0:T(8,128)(2,1)S(1)}, bf16[800,128]{1,0:T(8,128)(2,1)S(1)}, u32[]{:S(2)}, u32[]{:S(2)}) %collective-permute-start.1) | collective-permute-done | bytes 204832 | tf_op jit(solution)/shard_map/ppermute | solution.py:35
  66.6 1.9 collective-permute-start.2
  69.0 4.6 %collective-permute-start.9 = (bf16[800,128]{1,0:T(8,128)(2,1)S(1)}, bf16[800,128]{1,0:T(8,128)(2,1)S(1)}, u32[]{:S(2)}, u32[]{:S(2)}) collective-permute-start(bf16[800,128]{1,0:T(8,128)(2,1)S(1)} %collective-permute-done.8), channel_id=1, source_target_pairs={{0,15},{1,0},{2,1},{3,2},{4,3},{5,4},{6,5},{7,6},{8,7},{9,8},{10,9... | collective-permute-start | bytes 614408 | tf_op jit(solution)/shard_map/ppermute | solution.py:37
  74.8 1.9 collective-permute-start.3
  77.0 4.8 %collective-permute-start.10 = (bf16[800,128]{1,0:T(8,128)(2,1)S(1)}, bf16[800,128]{1,0:T(8,128)(2,1)S(1)}, u32[]{:S(2)}, u32[]{:S(2)}) collective-permute-start(bf16[800,128]{1,0:T(8,128)(2,1)S(1)} %collective-permute-done.9), channel_id=1, source_target_pairs={{0,15},{1,0},{2,1},{3,2},{4,3},{5,4},{6,5},{7,6},{8,7},{9,8},{10,9... | collective-permute-start | bytes 614408 | tf_op jit(solution)/shard_map/ppermute | solution.py:37
  82.9 1.9 collective-permute-start.4
  84.9 5.0 %collective-permute-start.11 = (bf16[800,128]{1,0:T(8,128)(2,1)S(1)}, bf16[800,128]{1,0:T(8,128)(2,1)S(1)}, u32[]{:S(2)}, u32[]{:S(2)}) collective-permute-start(bf16[800,128]{1,0:T(8,128)(2,1)S(1)} %collective-permute-done.10), channel_id=1, source_target_pairs={{0,15},{1,0},{2,1},{3,2},{4,3},{5,4},{6,5},{7,6},{8,7},{9,8},{10,9... | collective-permute-start | bytes 614408 | tf_op jit(solution)/shard_map/ppermute | solution.py:37
  90.6 1.9 collective-permute-start.5
  93.3 14.0 %all-to-all-start = ((s32[16,1,6]{2,1,0:T(1,128)}), s32[16,1,6]{2,1,0:T(1,128)S(1)}, u32[]{:S(2)}, u32[]{:S(2)}) async-start(s32[16,1,6]{2,1,0:T(1,128)} %copy.18), calls=%async_computation | async-start | bytes 16384 | tf_op jit(solution)/shard_map/all_to_all | solution.py:80
  107.3 4.9 %collective-permute-start.12 = (bf16[800,128]{1,0:T(8,128)(2,1)S(1)}, bf16[800,128]{1,0:T(8,128)(2,1)S(1)}, u32[]{:S(2)}, u32[]{:S(2)}) collective-permute-start(bf16[800,128]{1,0:T(8,128)(2,1)S(1)} %collective-permute-done.11), channel_id=1, source_target_pairs={{0,15},{1,0},{2,1},{3,2},{4,3},{5,4},{6,5},{7,6},{8,7},{9,8},{10,9... | collective-permute-start | bytes 614408 | tf_op jit(solution)/shard_map/ppermute | solution.py:37
  112.2 2.0 collective-permute-start.6
  114.3 1.9 collective-permute-done.12
  116.3 5.3 %collective-permute-start.13 = (bf16[800,128]{1,0:T(8,128)(2,1)S(1)}, bf16[800,128]{1,0:T(8,128)(2,1)S(1)}, u32[]{:S(2)}, u32[]{:S(2)}) collective-permute-start(bf16[800,128]{1,0:T(8,128)(2,1)S(1)} %collective-permute-done.12), channel_id=1, source_target_pairs={{0,15},{1,0},{2,1},{3,2},{4,3},{5,4},{6,5},{7,6},{8,7},{9,8},{10,9... | collective-permute-start | bytes 614408 | tf_op jit(solution)/shard_map/ppermute | solution.py:37
  121.6 2.0 collective-permute-start.7
  123.6 1.2 collective-permute-done.13
  124.8 5.5 %collective-permute-start.14 = (bf16[800,128]{1,0:T(8,128)(2,1)S(1)}, bf16[800,128]{1,0:T(8,128)(2,1)S(1)}, u32[]{:S(2)}, u32[]{:S(2)}) collective-permute-start(bf16[800,128]{1,0:T(8,128)(2,1)S(1)} %collective-permute-done.13), channel_id=1, source_target_pairs={{0,15},{1,0},{2,1},{3,2},{4,3},{5,4},{6,5},{7,6},{8,7},{9,8},{10,9... | collective-permute-start | bytes 614408 | tf_op jit(solution)/shard_map/ppermute | solution.py:37
  136.1 1.8 constant_dynamic-update-slice_fusion.23
  154.6 13.6 %fusion = bf16[256,8,16,128]{3,1,2,0:T(8,128)(2,1)} fusion(bf16[800,2048]{1,0:T(8,128)(2,1)} %all-gather.2.cloned.1.call-done, bf16[800,4096]{1,0:T(8,128)(2,1)} %constant_dynamic-update-slice_fusion, s32[]{:T(128)S(6)} %select_n.171), kind=kOutput, calls=%fused_computation.6 | convolution fusion | flops 6719275008 | bytes 14942212 | tf_op jit(solution)/shard_map/dot_general | solution.py:40
  168.2 9.7 %copy.22 = bf16[256,8,16,128]{3,2,1,0:T(8,128)(2,1)} copy(bf16[256,8,16,128]{3,1,2,0:T(8,128)(2,1)} %fusion) | data formatting | bytes 16777216
  178.0 9.1 %copy.24 = bf16[16,128,16,128]{3,1,2,0:T(8,128)(2,1)} copy(bf16[16,128,16,128]{3,2,1,0:T(8,128)(2,1)} %bitcast.35) | data formatting | bytes 16777216 | tf_op jit(solution)/shard_map/reshape | solution.py:48
  187.1 4.9 %gather_fusion.1 = bf16[96,128,128]{2,1,0:T(8,128)(2,1)S(1)} fusion(bf16[16,16,128,128]{3,2,1,0:T(8,128)(2,1)} %bitcast.36, s32[96]{0:T(128)S(1)} %reshape.311), kind=kCustom, calls=%fused_computation.1 | custom fusion | bytes 6292224 | tf_op jit(solution)/shard_map/gather | solution.py:75
  192.0 1.9 broadcast_select_fusion
  193.9 9.1 %all-to-all-start.1 = ((bf16[16,6,128,128]{3,2,1,0:T(8,128)(2,1)}), bf16[16,6,128,128]{3,2,1,0:T(8,128)(2,1)S(1)}, u32[]{:S(2)}, u32[]{:S(2)}) async-start(bf16[16,6,128,128]{3,2,1,0:T(8,128)(2,1)} %broadcast_select_fusion), calls=%async_computation.1 | async-start | bytes 6291456 | tf_op jit(solution)/shard_map/all_to_all | solution.py:79
  205.5 1.2 gather_fusion.3
  207.4 1.2 compare_select_fusion.6
  208.7 65.3 %all-to-all-done.1 = bf16[16,6,128,128]{3,2,1,0:T(8,128)(2,1)S(1)} async-done(((bf16[16,6,128,128]{3,2,1,0:T(8,128)(2,1)}), bf16[16,6,128,128]{3,2,1,0:T(8,128)(2,1)S(1)}, u32[]{:S(2)}, u32[]{:S(2)}) %all-to-all-start.1) | async-done | bytes 3145760 | tf_op jit(solution)/shard_map/all_to_all | solution.py:79
  274.0 2.7 gather_fusion.2
  276.7 3.4 %fusion.2 = bf16[1,1,96,128,128]{4,3,2,1,0:T(8,128)(2,1)} fusion(bf16[96,128,128]{2,1,0:T(8,128)(2,1)} %gather_fusion.2, pred[96]{0:T(512)(128)(4,1)S(1)} %get-tuple-element.8, pred[96]{0:T(512)(128)(4,1)S(1)} %get-tuple-element.9), kind=kLoop, calls=%fused_computation.9 | loop fusion | flops 3145728 | bytes 6291648 | tf_op jit(solution)/shard_map/jit(_where)/select_n | solution.py:19
  (89 shorter events, 34.2 us)
Async XLA Ops:
  7.2 51.0 %copy-start = (s32[16,16]{1,0:T(8,128)S(1)}, s32[16,16]{1,0:T(8,128)}, u32[]{:S(2)}) copy-start(s32[16,16]{1,0:T(8,128)} %param.4) | copy-start | bytes 3076
  7.2 141.6 %copy-start.1 = (f32[800,128]{1,0:T(8,128)S(1)}, f32[800,128]{1,0:T(8,128)}, u32[]{:S(2)}) copy-start(f32[800,128]{1,0:T(8,128)} %param.3) | copy-start | bytes 1228804
  7.2 147.4 %all-gather.2.cloned.1.call-start = ((), (), s32[]{:S(2)}) async-start(), calls=%async_computation.2 | async-start | bytes 3481600 | tf_op jit(solution)/shard_map/all_gather | solution.py:42
  10.6 46.5 %copy-start.2 = (bf16[800,128]{1,0:T(8,128)(2,1)}, bf16[800,128]{1,0:T(8,128)(2,1)S(1)}, u32[]{:S(2)}) copy-start(bf16[800,128]{1,0:T(8,128)(2,1)S(1)} %multiply_convert_fusion.1) | copy-start | bytes 614404
  10.6 48.3 %collective-permute-start = (bf16[800,128]{1,0:T(8,128)(2,1)S(1)}, bf16[800,128]{1,0:T(8,128)(2,1)S(1)}, u32[]{:S(2)}, u32[]{:S(2)}) collective-permute-start(bf16[800,128]{1,0:T(8,128)(2,1)S(1)} %multiply_convert_fusion.1), channel_id=1, source_target_pairs={{0,1},{1,2},{2,3},{3,4},{4,5},{5,6},{6,7},{7,8},{8,9},{9,10},{10,1... | collective-permute-start | bytes 614408 | tf_op jit(solution)/shard_map/ppermute | solution.py:35
  17.2 51.8 %collective-permute-start.8 = (bf16[800,128]{1,0:T(8,128)(2,1)S(1)}, bf16[800,128]{1,0:T(8,128)(2,1)S(1)}, u32[]{:S(2)}, u32[]{:S(2)}) collective-permute-start(bf16[800,128]{1,0:T(8,128)(2,1)S(1)} %multiply_convert_fusion.1), channel_id=1, source_target_pairs={{0,15},{1,0},{2,1},{3,2},{4,3},{5,4},{6,5},{7,6},{8,7},{9,8},{10,9... | collective-permute-start | bytes 614408 | tf_op jit(solution)/shard_map/ppermute | solution.py:37
  58.9 7.7 %collective-permute-start.1 = (bf16[800,128]{1,0:T(8,128)(2,1)S(1)}, bf16[800,128]{1,0:T(8,128)(2,1)S(1)}, u32[]{:S(2)}, u32[]{:S(2)}) collective-permute-start(bf16[800,128]{1,0:T(8,128)(2,1)S(1)} %collective-permute-done), channel_id=1, source_target_pairs={{0,1},{1,2},{2,3},{3,4},{4,5},{5,6},{6,7},{7,8},{8,9},{9,10},{10,1... | collective-permute-start | bytes 614408 | tf_op jit(solution)/shard_map/ppermute | solution.py:35
  66.6 8.1 %collective-permute-start.2 = (bf16[800,128]{1,0:T(8,128)(2,1)S(1)}, bf16[800,128]{1,0:T(8,128)(2,1)S(1)}, u32[]{:S(2)}, u32[]{:S(2)}) collective-permute-start(bf16[800,128]{1,0:T(8,128)(2,1)S(1)} %collective-permute-done.1), channel_id=1, source_target_pairs={{0,1},{1,2},{2,3},{3,4},{4,5},{5,6},{6,7},{7,8},{8,9},{9,10},{10,1... | collective-permute-start | bytes 614408 | tf_op jit(solution)/shard_map/ppermute | solution.py:35
  69.0 8.0 %collective-permute-start.9 = (bf16[800,128]{1,0:T(8,128)(2,1)S(1)}, bf16[800,128]{1,0:T(8,128)(2,1)S(1)}, u32[]{:S(2)}, u32[]{:S(2)}) collective-permute-start(bf16[800,128]{1,0:T(8,128)(2,1)S(1)} %collective-permute-done.8), channel_id=1, source_target_pairs={{0,15},{1,0},{2,1},{3,2},{4,3},{5,4},{6,5},{7,6},{8,7},{9,8},{10,9... | collective-permute-start | bytes 614408 | tf_op jit(solution)/shard_map/ppermute | solution.py:37
  74.8 8.1 %collective-permute-start.3 = (bf16[800,128]{1,0:T(8,128)(2,1)S(1)}, bf16[800,128]{1,0:T(8,128)(2,1)S(1)}, u32[]{:S(2)}, u32[]{:S(2)}) collective-permute-start(bf16[800,128]{1,0:T(8,128)(2,1)S(1)} %collective-permute-done.2), channel_id=1, source_target_pairs={{0,1},{1,2},{2,3},{3,4},{4,5},{5,6},{6,7},{7,8},{8,9},{9,10},{10,1... | collective-permute-start | bytes 614408 | tf_op jit(solution)/shard_map/ppermute | solution.py:35
  77.0 7.9 %collective-permute-start.10 = (bf16[800,128]{1,0:T(8,128)(2,1)S(1)}, bf16[800,128]{1,0:T(8,128)(2,1)S(1)}, u32[]{:S(2)}, u32[]{:S(2)}) collective-permute-start(bf16[800,128]{1,0:T(8,128)(2,1)S(1)} %collective-permute-done.9), channel_id=1, source_target_pairs={{0,15},{1,0},{2,1},{3,2},{4,3},{5,4},{6,5},{7,6},{8,7},{9,8},{10,9... | collective-permute-start | bytes 614408 | tf_op jit(solution)/shard_map/ppermute | solution.py:37
  82.9 7.7 %collective-permute-start.4 = (bf16[800,128]{1,0:T(8,128)(2,1)S(1)}, bf16[800,128]{1,0:T(8,128)(2,1)S(1)}, u32[]{:S(2)}, u32[]{:S(2)}) collective-permute-start(bf16[800,128]{1,0:T(8,128)(2,1)S(1)} %collective-permute-done.3), channel_id=1, source_target_pairs={{0,1},{1,2},{2,3},{3,4},{4,5},{5,6},{6,7},{7,8},{8,9},{9,10},{10,1... | collective-permute-start | bytes 614408 | tf_op jit(solution)/shard_map/ppermute | solution.py:35
  84.9 22.4 %collective-permute-start.11 = (bf16[800,128]{1,0:T(8,128)(2,1)S(1)}, bf16[800,128]{1,0:T(8,128)(2,1)S(1)}, u32[]{:S(2)}, u32[]{:S(2)}) collective-permute-start(bf16[800,128]{1,0:T(8,128)(2,1)S(1)} %collective-permute-done.10), channel_id=1, source_target_pairs={{0,15},{1,0},{2,1},{3,2},{4,3},{5,4},{6,5},{7,6},{8,7},{9,8},{10,9... | collective-permute-start | bytes 614408 | tf_op jit(solution)/shard_map/ppermute | solution.py:37
  90.6 21.5 %collective-permute-start.5 = (bf16[800,128]{1,0:T(8,128)(2,1)S(1)}, bf16[800,128]{1,0:T(8,128)(2,1)S(1)}, u32[]{:S(2)}, u32[]{:S(2)}) collective-permute-start(bf16[800,128]{1,0:T(8,128)(2,1)S(1)} %collective-permute-done.4), channel_id=1, source_target_pairs={{0,1},{1,2},{2,3},{3,4},{4,5},{5,6},{6,7},{7,8},{8,9},{9,10},{10,1... | collective-permute-start | bytes 614408 | tf_op jit(solution)/shard_map/ppermute | solution.py:35
  93.3 100.7 %all-to-all-start = ((s32[16,1,6]{2,1,0:T(1,128)}), s32[16,1,6]{2,1,0:T(1,128)S(1)}, u32[]{:S(2)}, u32[]{:S(2)}) async-start(s32[16,1,6]{2,1,0:T(1,128)} %copy.18), calls=%async_computation | async-start | bytes 16384 | tf_op jit(solution)/shard_map/all_to_all | solution.py:80
  107.3 9.0 %collective-permute-start.12 = (bf16[800,128]{1,0:T(8,128)(2,1)S(1)}, bf16[800,128]{1,0:T(8,128)(2,1)S(1)}, u32[]{:S(2)}, u32[]{:S(2)}) collective-permute-start(bf16[800,128]{1,0:T(8,128)(2,1)S(1)} %collective-permute-done.11), channel_id=1, source_target_pairs={{0,15},{1,0},{2,1},{3,2},{4,3},{5,4},{6,5},{7,6},{8,7},{9,8},{10,9... | collective-permute-start | bytes 614408 | tf_op jit(solution)/shard_map/ppermute | solution.py:37
  112.2 9.4 %collective-permute-start.6 = (bf16[800,128]{1,0:T(8,128)(2,1)S(1)}, bf16[800,128]{1,0:T(8,128)(2,1)S(1)}, u32[]{:S(2)}, u32[]{:S(2)}) collective-permute-start(bf16[800,128]{1,0:T(8,128)(2,1)S(1)} %collective-permute-done.5), channel_id=1, source_target_pairs={{0,1},{1,2},{2,3},{3,4},{4,5},{5,6},{6,7},{7,8},{8,9},{9,10},{10,1... | collective-permute-start | bytes 614408 | tf_op jit(solution)/shard_map/ppermute | solution.py:35
  116.3 8.6 %collective-permute-start.13 = (bf16[800,128]{1,0:T(8,128)(2,1)S(1)}, bf16[800,128]{1,0:T(8,128)(2,1)S(1)}, u32[]{:S(2)}, u32[]{:S(2)}) collective-permute-start(bf16[800,128]{1,0:T(8,128)(2,1)S(1)} %collective-permute-done.12), channel_id=1, source_target_pairs={{0,15},{1,0},{2,1},{3,2},{4,3},{5,4},{6,5},{7,6},{8,7},{9,8},{10,9... | collective-permute-start | bytes 614408 | tf_op jit(solution)/shard_map/ppermute | solution.py:37
  121.6 8.7 %collective-permute-start.7 = (bf16[800,128]{1,0:T(8,128)(2,1)S(1)}, bf16[800,128]{1,0:T(8,128)(2,1)S(1)}, u32[]{:S(2)}, u32[]{:S(2)}) collective-permute-start(bf16[800,128]{1,0:T(8,128)(2,1)S(1)} %collective-permute-done.6), channel_id=1, source_target_pairs={{0,1},{1,2},{2,3},{3,4},{4,5},{5,6},{6,7},{7,8},{8,9},{9,10},{10,1... | collective-permute-start | bytes 614408 | tf_op jit(solution)/shard_map/ppermute | solution.py:35
  124.8 17.4 %collective-permute-start.14 = (bf16[800,128]{1,0:T(8,128)(2,1)S(1)}, bf16[800,128]{1,0:T(8,128)(2,1)S(1)}, u32[]{:S(2)}, u32[]{:S(2)}) collective-permute-start(bf16[800,128]{1,0:T(8,128)(2,1)S(1)} %collective-permute-done.13), channel_id=1, source_target_pairs={{0,15},{1,0},{2,1},{3,2},{4,3},{5,4},{6,5},{7,6},{8,7},{9,8},{10,9... | collective-permute-start | bytes 614408 | tf_op jit(solution)/shard_map/ppermute | solution.py:37
  193.9 80.0 %all-to-all-start.1 = ((bf16[16,6,128,128]{3,2,1,0:T(8,128)(2,1)}), bf16[16,6,128,128]{3,2,1,0:T(8,128)(2,1)S(1)}, u32[]{:S(2)}, u32[]{:S(2)}) async-start(bf16[16,6,128,128]{3,2,1,0:T(8,128)(2,1)} %broadcast_select_fusion), calls=%async_computation.1 | async-start | bytes 6291456 | tf_op jit(solution)/shard_map/all_to_all | solution.py:79
Sparse Core Ops, SparseCore 0:
  57.4 46.6 all-gather.1
